TPU v7x, 512 devices: a 8x2x16 block of a 8x16x16 slice. The times are simulated.
512 devices in a mesh: groups: 2 (over y), seq: 32 (over z, core), rep: 8 (over x).
Axes of the slice: x: 8, y: 2, z: 16, core: 2. Of those that a mesh axis runs over, the one named last changes fastest.
The devices are a block of a 8x16x16 slice.
Arguments:
- queries: bfloat16 [1024, 4096], P(('groups', 'seq'), 'rep'), parts along dimension 0, may hold values from -128 to 128
- keys_new: bfloat16 [1024, 1024], P(('groups', 'seq'), 'rep'), parts along dimension 0, may hold values from -4 to 4
- values_new: bfloat16 [1024, 1024], P(('groups', 'seq'), 'rep'), parts along dimension 0, may hold values from -6 to 6
- keys_past: bfloat16 [16384, 1024], P(('groups', 'seq'), 'rep'), parts along dimension 0, may hold values from -4 to 4
- values_past: bfloat16 [16384, 1024], P(('groups', 'seq'), 'rep'), parts along dimension 0, may hold values from -6 to 6
- block_order: int32 [64], P('groups'), parts along dimension 0, may hold values from 0 to 31, each once
- residual: bfloat16 [1024, 4096], P(('groups', 'seq'), 'rep'), parts along dimension 0, may hold values from -6 to 6
- out_proj: bfloat16 [4096, 4096], P('seq', 'rep'), may hold values from -0.09375 to 0.09375
- norm_gain: float32 [4096], replicated, may hold values from 0.5 to 1.5
- router: float32 [4096, 4], replicated, may hold values from -0.09375 to 0.09375
- w_gate: bfloat16 [8, 4096, 4096], P('rep', None, 'seq'), may hold values from -0.09375 to 0.09375
- w_up: bfloat16 [8, 4096, 4096], P('rep', None, 'seq'), may hold values from -0.09375 to 0.09375
- w_down: bfloat16 [8, 4096, 4096], P('rep', 'seq'), may hold values from -0.0625 to 0.0625
- expert_ids: int32 [1024, 2], P(('groups', 'seq')), parts along dimension 0, may hold values from 0 to 3, all different within a row; in each aligned block of 16 rows (0 to 15, 16 to 31, ...) at most 12 rows name the same one
Outputs:
- attended: bfloat16 [1024, 4096], P(('groups', 'seq'), 'rep'), parts along dimension 0
- layer_out: bfloat16 [1024, 4096], P(('groups', 'seq'), 'rep'), parts along dimension 0
- keys_cache: bfloat16 [1024, 1024], P(('groups', 'seq')), parts along dimension 0
- values_cache: bfloat16 [1024, 1024], P(('groups', 'seq')), parts along dimension 0
There are 2 independent parts, one for each index of `groups`. A program takes and returns all parts, laid end to end along the dimension named above; an argument that names none is the same for every part. Nothing has to cross between parts.
Inputs may be any that keep to these rules, and one draw needn't show every extreme that they name: `block_order`: each block index 0 to 32 - 1 appears once. `expert_ids`: each row names 2 different experts; in the rows of one device (aligned blocks of 16 rows) no expert is named by more than 12 rows, and in some block one expert is named by exactly 12.
All inputs are finite; a program needn't handle non-finite values.
Results may differ from a plain program's by a relative error of at most 0.011.
Values may be sent and summed in bfloat16 or wider, within the bound.
A program may use at most 64 MiB of HBM per device.

v0:
```python
import math
import jax
import jax.numpy as jnp
from jax import lax
from jax.sharding import Mesh
from jax.sharding import PartitionSpec as P

EXPERTS = 4
CAP = 12
SEQ = ("seq_0", "seq_1")
GROUPS_SEQ = ("groups", "seq_0", "seq_1")


def in_one_piece(arrays, axis, dim, along):
    both = jnp.concatenate(arrays, axis=along)
    out, at, gathered = (lax.all_gather(both, axis, axis=dim, tiled=True), 0, [])
    for a in arrays:
        gathered.append(lax.slice_in_dim(out, at, at + a.shape[along], axis=along))
        at += a.shape[along]
    return tuple(gathered)


def sent_to_all(array, axis):
    size = lax.axis_size(axis)
    return lax.all_to_all(
        jnp.broadcast_to(array[None], (size, *array.shape)), axis, 0, 0, tiled=True
    )


def laid_out(tiles, dim):
    tiles = jnp.moveaxis(tiles, 0, dim)
    shape = tiles.shape
    return tiles.reshape(*shape[:dim], shape[dim] * shape[dim + 1], *shape[dim + 2 :])


def gather_directly(array, axis, dim):
    tiles = sent_to_all(array, axis)
    return laid_out(tiles, dim)


def own_block(tiles, axes, order):
    shape = [lax.axis_size(a) for a in axes]
    tiles = tiles.reshape(*shape, *tiles.shape[1:])
    tiles = tiles.transpose(*order, *range(len(axes), tiles.ndim))
    tiles = tiles.reshape(-1, *tiles.shape[len(axes) :])
    for k in order:
        tiles = lax.psum_scatter(tiles, axes[k], scatter_dimension=0, tiled=True)
    return tiles[0]


def in_blocks(array, dim, size):
    shape = array.shape
    tiles = array.reshape(*shape[:dim], size, shape[dim] // size, *shape[dim + 1 :])
    return jnp.moveaxis(tiles, dim, 0)


def sum_by_axis(array, axes, order, dim):
    size = lax.axis_size(axes)
    return own_block(in_blocks(array, dim, size), axes, order)


def block_lookup(owners, block_order):
    width = block_order.shape[0]
    hits = owners[:, None] == jnp.arange(width, dtype=jnp.int32)[None, :]
    return jnp.sum(jnp.where(hits, block_order[None, :], 0), axis=1)


def body(
    queries,
    keys_new,
    values_new,
    keys_past,
    values_past,
    block_order,
    residual,
    out_proj,
    norm_gain,
    router,
    w_gate,
    w_up,
    w_down,
    expert_ids,
):
    seq_index = lax.axis_index(SEQ)
    rep_index = lax.axis_index("rep")
    rep_count = lax.axis_size("rep")
    tok_count = queries.shape[0]
    head_dim = keys_new.shape[1]
    q_per = queries.shape[1] // head_dim
    past_len = keys_past.shape[0]
    key_span = past_len + tok_count
    row_total = tok_count * q_per
    my_block = block_lookup(jnp.full((1,), seq_index, jnp.int32), block_order)[0]
    scaling = 1.0 / math.sqrt(head_dim)
    query_rows = queries.reshape(row_total, head_dim)
    query_pos = my_block * tok_count + jnp.arange(row_total, dtype=jnp.int32) // q_per
    keys_local = jnp.concatenate([keys_past, keys_new], axis=0)
    values_local = jnp.concatenate([values_past, values_new], axis=0)
    running = jnp.full((row_total,), -1e30, jnp.float32)
    key_piece, value_piece = in_one_piece((keys_local, values_local), SEQ, 0, 1)
    row_count = key_piece.shape[0]
    key_index = jnp.arange(row_count, dtype=jnp.int32)
    key_owner = key_index // key_span
    offset = key_index % key_span
    key_pos = block_lookup(key_owner, block_order) * tok_count + offset - past_len
    visible = (offset < past_len)[None, :] | (key_pos[None, :] <= query_pos[:, None])
    scores = jnp.dot(query_rows, key_piece.T, preferred_element_type=jnp.float32) * scaling
    highest = jnp.maximum(running, jnp.max(jnp.where(visible, scores, -1e30), axis=1))
    weights = jnp.where(visible, jnp.exp(scores - highest[:, None]), 0.0)
    totals = jnp.sum(weights, axis=1)
    numerator = jnp.dot(
        weights.astype(jnp.bfloat16), value_piece, preferred_element_type=jnp.float32
    )
    running, totals, numerator = (highest, totals, numerator)
    attn_local = (
        (numerator / totals[:, None]).reshape(tok_count, q_per * head_dim).astype(jnp.bfloat16)
    )
    attn_full, keys_cache, values_cache = (
        lax.all_gather(attn_local, "rep", axis=1, tiled=True),
        *in_one_piece((keys_new, values_new), "rep", 1, 0),
    )
    projected = jnp.dot(
        attn_full,
        lax.all_gather(out_proj, SEQ, axis=0, tiled=True),
        preferred_element_type=jnp.float32,
    )
    attended = (residual.astype(jnp.float32) + projected).astype(jnp.bfloat16)
    full_rows = gather_directly(attended, "rep", 1)
    features = full_rows.astype(jnp.float32)
    mean_square = jnp.mean(features * features, axis=1, keepdims=True)
    normed = (features * norm_gain[None, :] * lax.rsqrt(mean_square + 1e-05)).astype(jnp.bfloat16)
    logits = jnp.dot(normed.astype(jnp.float32), router, precision=lax.Precision.HIGHEST)
    expert_range = jnp.arange(EXPERTS, dtype=jnp.int32)
    first_pick = (expert_ids[:, 0:1] == expert_range[None, :]).astype(jnp.float32)
    second_pick = (expert_ids[:, 1:2] == expert_range[None, :]).astype(jnp.float32)
    share_first = jax.nn.sigmoid(
        jnp.sum(first_pick * logits, axis=1) - jnp.sum(second_pick * logits, axis=1)
    )
    token_share = share_first[:, None] * first_pick + (1.0 - share_first)[:, None] * second_pick
    member = first_pick + second_pick
    ranking = jnp.cumsum(member, axis=0) - member
    slot_range = jnp.arange(CAP, dtype=jnp.float32)
    selection = member.T[:, None, :] * (ranking.T[:, None, :] == slot_range[None, :, None]).astype(
        jnp.float32
    )
    mine_mask = (expert_range == rep_index % EXPERTS).astype(jnp.float32)
    my_selection = jnp.einsum("e,ejt->jt", mine_mask, selection)
    slot_rows = jnp.dot(
        my_selection.astype(jnp.bfloat16), normed, preferred_element_type=jnp.float32
    ).astype(jnp.bfloat16)
    gate_local = w_gate[0]
    up_local = w_up[0]
    down_local = w_down[0]
    piece = lax.all_gather(slot_rows, SEQ, axis=0, tiled=True)
    gate_part = jnp.dot(piece, gate_local, preferred_element_type=jnp.float32)
    up_part = jnp.dot(piece, up_local, preferred_element_type=jnp.float32)
    hidden_slots = (jax.nn.silu(gate_part) * up_part).astype(jnp.bfloat16)
    expert_part = sum_by_axis(
        jnp.dot(hidden_slots, down_local, preferred_element_type=jnp.float32).astype(jnp.bfloat16),
        SEQ,
        (1, 0),
        0,
    ).astype(jnp.float32)
    returned = lax.all_to_all(
        expert_part.astype(jnp.bfloat16), "rep", split_axis=1, concat_axis=0, tiled=True
    ).astype(expert_part.dtype)
    source_expert = jnp.arange(rep_count, dtype=jnp.int32) % EXPERTS
    source_pick = (source_expert[:, None] == expert_range[None, :]).astype(jnp.float32)
    combine = jnp.einsum("re,ejt,te->trj", source_pick, selection, token_share).reshape(
        tok_count, rep_count * CAP
    )
    moe_slice = jnp.dot(combine, returned, precision=lax.Precision.HIGHEST)
    layer_out = (attended.astype(jnp.float32) + moe_slice).astype(jnp.bfloat16)
    return (attended, layer_out, keys_cache, values_cache)


def solution(mesh):
    split = Mesh(
        mesh.devices.reshape(mesh.shape["groups"], 16, 2, mesh.shape["rep"]),
        ("groups", "seq_0", "seq_1", "rep"),
    )
    return jax.shard_map(
        body,
        mesh=split,
        in_specs=(
            P(GROUPS_SEQ, "rep"),
            P(GROUPS_SEQ, "rep"),
            P(GROUPS_SEQ, "rep"),
            P(GROUPS_SEQ, "rep"),
            P(GROUPS_SEQ, "rep"),
            P("groups"),
            P(GROUPS_SEQ, "rep"),
            P(SEQ, "rep"),
            P(),
            P(),
            P("rep", None, SEQ),
            P("rep", None, SEQ),
            P("rep", SEQ, None),
            P(GROUPS_SEQ, None),
        ),
        out_specs=(
            P(GROUPS_SEQ, "rep"),
            P(GROUPS_SEQ, "rep"),
            P(GROUPS_SEQ, None),
            P(GROUPS_SEQ, None),
        ),
        check_vma=False,
    )
```

profile of v0, /device:TPU:66, one launch (start us, length us, event | category | flops | bytes accessed | tf_op | source)
XLA Modules:
  0.0 435.2 jit_solution(9324647808169427397)
XLA Ops:
  7.3 1.7 maximum_maximum_fusion
  10.5 1.3 fusion.64
  12.5 0.9 select_reduce_fusion.1
  13.5 106.4 %all-gather.5.cloned.1.call-done = bf16[8704,256]{1,0:T(8,128)(2,1)} async-done(((bf16[272,256]{1,0:T(8,128)(2,1)}), bf16[8704,256]{1,0:T(8,128)(2,1)}) %all-gather.5.cloned.1.call-update) | async-done | bytes 4456464 | tf_op jit(solution)/shard_map/all_gather | solution.py:16
  119.9 2.8 select_reduce_fusion
  124.5 24.7 %all_gather.16 = bf16[16,4096]{1,0:T(8,128)(2,1)S(1)} all-gather(bf16[16,512]{1,0:T(8,128)(2,1)S(1)} %convert_element_type.81), channel_id=1, replica_groups=mesh['groups'=2,'seq_0'=16,'seq_1'=2,'rep'=8] {'rep'}, dimensions={1}, use_global_device_ids=true | all-gather | bytes 147456 | tf_op jit(solution)/shard_map/all_gather | solution.py:119
  149.2 44.8 %all-gather.7.cloned.1.call-done = bf16[4096,512]{1,0:T(8,128)(2,1)} async-done(((bf16[128,512]{1,0:T(8,128)(2,1)}), bf16[4096,512]{1,0:T(8,128)(2,1)}) %all-gather.7.cloned.1.call-update) | async-done | bytes 4194320 | tf_op jit(solution)/shard_map/all_gather | solution.py:124
  194.0 2.8 fusion.16
  197.5 7.2 %all-to-all-start = ((bf16[8,16,512]{2,1,0:T(8,128)(2,1)}), bf16[8,16,512]{2,1,0:T(8,128)(2,1)S(1)}, u32[]{:S(2)}, u32[]{:S(2)}) async-start(bf16[8,16,512]{2,1,0:T(8,128)(2,1)} %broadcast_in_dim.33), calls=%async_computation | async-start | bytes 262144 | tf_op jit(solution)/shard_map/all_to_all | solution.py:25
  204.8 8.0 %all-to-all-done = bf16[8,16,512]{2,1,0:T(8,128)(2,1)S(1)} async-done(((bf16[8,16,512]{2,1,0:T(8,128)(2,1)}), bf16[8,16,512]{2,1,0:T(8,128)(2,1)S(1)}, u32[]{:S(2)}, u32[]{:S(2)}) %all-to-all-start) | async-done | bytes 131104 | tf_op jit(solution)/shard_map/all_to_all | solution.py:25
  213.7 0.9 fusion.1
  214.7 68.2 %all-gather.9.cloned.1.call-done = bf16[32,12,4096]{2,1,0:T(8,128)(2,1)} async-done(((bf16[1,12,4096]{2,1,0:T(8,128)(2,1)}), bf16[32,12,4096]{2,1,0:T(8,128)(2,1)}) %all-gather.9.cloned.1.call-update) | async-done | bytes 3145744 | tf_op jit(solution)/shard_map/all_gather | solution.py:154
  282.9 5.6 %reshape.160 = bf16[384,4096]{1,0:T(8,128)(2,1)} reshape(bf16[32,12,4096]{2,1,0:T(8,128)(2,1)} %all-gather.9.cloned.1.call-done) | data formatting | bytes 6291456
  288.5 2.9 fusion.30
  291.5 7.0 %convolution_convert_fusion = bf16[384,4096]{1,0:T(8,128)(2,1)} fusion(bf16[384,4096]{1,0:T(8,128)(2,1)} %reshape.160, bf16[1,128,4096]{2,1,0:T(8,128)(2,1)S(1)} %copy-done, bf16[1,4096,128]{2,1,0:T(8,128)(2,1)S(1)} %copy-done.2, f32[384,128]{1,0:T(8,128)S(1)} %fusion.30), kind=kOutput, calls=%fused_computation.2 | convolution fusion | flops 807174144 | bytes 8585216 | tf_op jit(solution)/shard_map/dot_general | solution.py:159
  298.5 5.5 %reshape_reshape.3 = bf16[16,2,12,4096]{3,2,1,0:T(8,128)(2,1)} reshape(bf16[384,4096]{1,0:T(8,128)(2,1)} %convolution_convert_fusion) | data formatting | bytes 6291456 | tf_op jit(solution)/shard_map/reshape;reshape | solution.py:43
  304.0 5.6 %copy.51 = bf16[2,16,12,4096]{3,1,0,2:T(8,128)(2,1)} copy(bf16[2,16,12,4096]{3,2,0,1:T(8,128)(2,1)} %bitcast.62) | data formatting | bytes 6291456 | tf_op jit(solution)/shard_map/transpose | solution.py:44
  309.9 19.5 %reduce-scatter.3.cloned.1.call-done = bf16[16,12,4096]{2,0,1:T(8,128)(2,1)} async-done(((bf16[32,12,4096]{2,0,1:T(8,128)(2,1)}), bf16[16,12,4096]{2,0,1:T(8,128)(2,1)}) %reduce-scatter.3.cloned.1.call-update) | async-done | bytes 1572880 | tf_op jit(solution)/shard_map/reduce_scatter | solution.py:47
  329.5 3.7 copy.52
  333.2 22.3 %all_gather.19 = bf16[32,1024]{1,0:T(8,128)(2,1)S(1)} all-gather(bf16[32,128]{1,0:T(8,128)(2,1)S(1)} %pad_maximum_fusion), channel_id=1, replica_groups=mesh['groups'=2,'seq_0'=16,'seq_1'=2,'rep'=8] {'rep'}, dimensions={1}, use_global_device_ids=true | all-gather | bytes 73728 | tf_op jit(solution)/shard_map/all_gather | solution.py:16
  356.2 54.9 %reduce-scatter.5.cloned.1.call-done = bf16[1,12,4096]{2,1,0:T(8,128)(2,1)} async-done(((bf16[16,12,4096]{2,1,0:T(8,128)(2,1)}), bf16[1,12,4096]{2,1,0:T(8,128)(2,1)}) %reduce-scatter.5.cloned.1.call-update) | async-done | bytes 98320 | tf_op jit(solution)/shard_map/reduce_scatter | solution.py:47
  411.1 0.9 copy.57
  412.7 7.4 %all-to-all-start.1 = ((bf16[12,8,512]{2,0,1:T(8,128)(2,1)}), bf16[12,8,512]{2,0,1:T(8,128)(2,1)S(1)}, u32[]{:S(2)}, u32[]{:S(2)}) async-start(bf16[12,8,512]{2,0,1:T(8,128)(2,1)} %copy.53), calls=%async_computation.3 | async-start | bytes 262144 | tf_op jit(solution)/shard_map/all_to_all | solution.py:164
  420.4 7.4 %all-to-all-done.1 = bf16[12,8,512]{2,0,1:T(8,128)(2,1)S(1)} async-done(((bf16[12,8,512]{2,0,1:T(8,128)(2,1)}), bf16[12,8,512]{2,0,1:T(8,128)(2,1)S(1)}, u32[]{:S(2)}, u32[]{:S(2)}) %all-to-all-start.1) | async-done | bytes 98336 | tf_op jit(solution)/shard_map/all_to_all | solution.py:164
  (62 shorter events, 7.9 us)
Async XLA Ops:
  7.2 284.3 %copy-start = (bf16[1,128,4096]{2,1,0:T(8,128)(2,1)S(1)}, bf16[1,128,4096]{2,1,0:T(8,128)(2,1)}, u32[]{:S(2)}) copy-start(bf16[1,128,4096]{2,1,0:T(8,128)(2,1)} %param.26) | copy-start | bytes 3145732
  7.2 112.7 %all-gather.5.cloned.1.call-start = ((), (), s32[]{:S(2)}) async-start(), calls=%async_computation.4 | async-start | bytes 4595712 | tf_op jit(solution)/shard_map/all_gather | solution.py:16
  9.0 185.0 %all-gather.7.cloned.1.call-start = ((), (), s32[]{:S(2)}) async-start(), calls=%async_computation.5 | async-start | bytes 4325376 | tf_op jit(solution)/shard_map/all_gather | solution.py:124
  119.9 3.7 copy-start.10
  123.6 70.4 %copy-start.6 = (bf16[16,512]{1,0:T(8,128)(2,1)S(1)}, bf16[16,512]{1,0:T(8,128)(2,1)}, u32[]{:S(2)}) copy-start(bf16[16,512]{1,0:T(8,128)(2,1)} %param.20) | copy-start | bytes 49156
  149.2 55.5 %copy-start.9 = (s32[16,2]{0,1:T(2,128)S(1)}, s32[16,2]{0,1:T(2,128)}, u32[]{:S(2)}) copy-start(s32[16,2]{0,1:T(2,128)} %param.27) | copy-start | bytes 388
  149.2 63.7 %copy-start.4 = (f32[4096,4]{0,1:T(4,128)S(1)}, f32[4096,4]{0,1:T(4,128)}, u32[]{:S(2)}) copy-start(f32[4096,4]{0,1:T(4,128)} %param.23) | copy-start | bytes 196612
  149.2 63.8 %copy-start.5 = (f32[4096]{0:T(1024)S(1)}, f32[4096]{0:T(1024)}, u32[]{:S(2)}) copy-start(f32[4096]{0:T(1024)} %param.22) | copy-start | bytes 49156
  196.8 231.0 %copy-start.3 = (bf16[16,512]{1,0:T(8,128)(2,1)}, bf16[16,512]{1,0:T(8,128)(2,1)S(1)}, u32[]{:S(2)}) copy-start(bf16[16,512]{1,0:T(8,128)(2,1)S(1)} %fusion.16) | copy-start | bytes 49156
  197.5 15.2 %all-to-all-start = ((bf16[8,16,512]{2,1,0:T(8,128)(2,1)}), bf16[8,16,512]{2,1,0:T(8,128)(2,1)S(1)}, u32[]{:S(2)}, u32[]{:S(2)}) async-start(bf16[8,16,512]{2,1,0:T(8,128)(2,1)} %broadcast_in_dim.33), calls=%async_computation | async-start | bytes 262144 | tf_op jit(solution)/shard_map/all_to_all | solution.py:25
  204.7 78.2 %all-gather.9.cloned.1.call-start = ((), (), s32[]{:S(2)}) async-start(), calls=%async_computation.8 | async-start | bytes 4325376 | tf_op jit(solution)/shard_map/all_gather | solution.py:154
  214.6 73.9 %copy-start.1 = (bf16[1,4096,128]{2,1,0:T(8,128)(2,1)S(1)}, bf16[1,4096,128]{2,1,0:T(8,128)(2,1)}, u32[]{:S(2)}) copy-start(bf16[1,4096,128]{2,1,0:T(8,128)(2,1)} %param.24) | copy-start | bytes 3145732
  214.6 114.8 %reduce-scatter.3.cloned.1.call-start = ((), (), s32[]{:S(2)}) async-start(), calls=%async_computation.6 | async-start | bytes 4718592 | tf_op jit(solution)/shard_map/reduce_scatter | solution.py:47
  288.5 3.0 copy-start.2
  309.7 23.5 %copy-start.7 = (bf16[16,128]{1,0:T(8,128)(2,1)S(1)}, bf16[16,128]{1,0:T(8,128)(2,1)}, u32[]{:S(2)}) copy-start(bf16[16,128]{1,0:T(8,128)(2,1)} %param.16) | copy-start | bytes 12292
  309.7 23.5 %copy-start.8 = (bf16[16,128]{1,0:T(8,128)(2,1)S(1)}, bf16[16,128]{1,0:T(8,128)(2,1)}, u32[]{:S(2)}) copy-start(bf16[16,128]{1,0:T(8,128)(2,1)} %param.15) | copy-start | bytes 12292
  309.7 101.4 %reduce-scatter.5.cloned.1.call-start = ((), (), s32[]{:S(2)}) async-start(), calls=%async_computation.7 | async-start | bytes 2228224 | tf_op jit(solution)/shard_map/reduce_scatter | solution.py:47
  412.7 15.1 %all-to-all-start.1 = ((bf16[12,8,512]{2,0,1:T(8,128)(2,1)}), bf16[12,8,512]{2,0,1:T(8,128)(2,1)S(1)}, u32[]{:S(2)}, u32[]{:S(2)}) async-start(bf16[12,8,512]{2,0,1:T(8,128)(2,1)} %copy.53), calls=%async_computation.3 | async-start | bytes 262144 | tf_op jit(solution)/shard_map/all_to_all | solution.py:164
Sparse Core Ops, SparseCore 0:
  10.2 109.7 all-gather.4
  122.1 71.8 all-gather.6
  214.7 68.1 all-gather.8
  309.8 19.6 reduce-scatter.2
  333.3 77.7 reduce-scatter.4
where the time goes:
time: 436 us; the launch traced here: 435 us
  waiting for transfers between devices  310 us (71%)
  blocking collectives  47 us (11%)
  local copies, waits for them, and re-layouts  24.3 us (6%)
  matrix products  18.8 us (4%)
  starting transfers between devices  15.1 us (3%)
  between operations  14.7 us (3%)
  other arithmetic  5.04 us (1%)
    all_gather x1, waiting for transfers between devices, in_one_piece(): lax.all_gather(both, axis, axis=dim, tiled=True)  106 us
    reduce_scatter x2, waiting for transfers between devices, own_block(): tiles = lax.psum_scatter(tiles, axes[k], scatter_dimension=0, tiled=True)  74.4 us
    all_gather x1, waiting for transfers between devices, body(): piece = lax.all_gather(slot_rows, SEQ, axis=0, tiled=True)  68.2 us
    all_gather x1, waiting for transfers between devices, body(): lax.all_gather(out_proj, SEQ, axis=0, tiled=True)  44.8 us
    all_gather x1, blocking collectives, body(): lax.all_gather(attn_local, 'rep', axis=1, tiled=True)  24.7 us
    all_gather x1, blocking collectives, in_one_piece(): lax.all_gather(both, axis, axis=dim, tiled=True)  22.3 us
  transfers between devices with their start and end apart: 7, of which 7 were waited for; matrix products, arithmetic and copies ran while one was open for 2% of the time, Pallas kernels for 0%

commit v1 on v0

--- a/solution.py
+++ b/solution.py
@@ -9,6 +9,18 @@
 CAP = 12
 SEQ = ("seq_0", "seq_1")
 GROUPS_SEQ = ("groups", "seq_0", "seq_1")
+
+
+def gather_by_bits(x, axis, dim):
+    ways, here = (lax.axis_size(axis), lax.axis_index(axis))
+    grown, reach = (x, 1)
+    while reach < ways:
+        theirs = lax.ppermute(grown, axis, [(d, d ^ reach) for d in range(ways)])
+        mine_first = jnp.concatenate([grown, theirs], axis=dim)
+        theirs_first = jnp.concatenate([theirs, grown], axis=dim)
+        grown = jnp.where(here & reach == 0, mine_first, theirs_first)
+        reach = 2 * reach
+    return grown
 
 
 def in_one_piece(arrays, axis, dim, along):
@@ -116,7 +128,7 @@
         (numerator / totals[:, None]).reshape(tok_count, q_per * head_dim).astype(jnp.bfloat16)
     )
     attn_full, keys_cache, values_cache = (
-        lax.all_gather(attn_local, "rep", axis=1, tiled=True),
+        gather_by_bits(attn_local, "rep", 1),
         *in_one_piece((keys_new, values_new), "rep", 1, 0),
     )
     projected = jnp.dot(

time: 436 us -> 436 us (level)
  blocking collectives: 47 us -> 22.4 us
  starting transfers between devices: 15.1 us -> 28.1 us
  waiting for transfers between devices: 310 us -> 322 us
    all_gather x1 -> x0, blocking collectives: 24.7 us -> none  [body(): lax.all_gather(attn_local, 'rep', axis=1, tiled=True)]
    ppermute x0 -> x3, starting transfers between devices: none -> 13.4 us  [gather_by_bits(): theirs = lax.ppermute(grown, axis, [(d, d ^ reach) for d in range(ways)])]
    all_gather x1, waiting for transfers between devices: 44.8 us -> 50.7 us  [body(): lax.all_gather(out_proj, SEQ, axis=0, tiled=True)]
    ppermute x0 -> x3, waiting for transfers between devices: none -> 5.56 us  [gather_by_bits(): theirs = lax.ppermute(grown, axis, [(d, d ^ reach) for d in range(ways)])]
  transfers between devices with their start and end apart: 7 -> 10, of which waited for: 7 -> 9; matrix products, arithmetic and copies ran while one was open for 2% -> 2% of each run, Pallas kernels for 0% -> 0%
where the time goes in v1:
time: 436 us; the launch traced here: 435 us
  waiting for transfers between devices  322 us (74%)
  starting transfers between devices  28.1 us (6%)
  local copies, waits for them, and re-layouts  24.2 us (6%)
  blocking collectives  22.4 us (5%)
  matrix products  18.8 us (4%)
  between operations  14.8 us (3%)
  other arithmetic  5.06 us (1%)
    all_gather x1, waiting for transfers between devices, in_one_piece(): lax.all_gather(both, axis, axis=dim, tiled=True)  106 us
    reduce_scatter x2, waiting for transfers between devices, own_block(): tiles = lax.psum_scatter(tiles, axes[k], scatter_dimension=0, tiled=True)  74.5 us
    all_gather x1, waiting for transfers between devices, body(): piece = lax.all_gather(slot_rows, SEQ, axis=0, tiled=True)  68.3 us
    all_gather x1, waiting for transfers between devices, body(): lax.all_gather(out_proj, SEQ, axis=0, tiled=True)  50.7 us
    all_gather x1, blocking collectives, in_one_piece(): lax.all_gather(both, axis, axis=dim, tiled=True)  22.4 us
    ppermute x3, starting transfers between devices, gather_by_bits(): theirs = lax.ppermute(grown, axis, [(d, d ^ reach) for d in range(ways)])  13.4 us
  transfers between devices with their start and end apart: 10, of which 9 were waited for; matrix products, arithmetic and copies ran while one was open for 2% of the time, Pallas kernels for 0%

profile of v1, /device:TPU:66, one launch (start us, length us, event | category | flops | bytes accessed | tf_op | source)
XLA Modules:
  0.0 435.1 jit_solution(6313346168963385590)
XLA Ops:
  7.3 1.7 maximum_maximum_fusion
  13.5 106.4 %all-gather.5.cloned.1.call-done = bf16[8704,256]{1,0:T(8,128)(2,1)} async-done(((bf16[272,256]{1,0:T(8,128)(2,1)}), bf16[8704,256]{1,0:T(8,128)(2,1)}) %all-gather.5.cloned.1.call-update) | async-done | bytes 4456464 | tf_op jit(solution)/shard_map/all_gather | solution.py:28
  119.9 2.8 select_reduce_fusion
  124.5 2.5 collective-permute-start
  127.0 3.2 collective-permute-done
  130.2 4.3 collective-permute-start.1
  134.5 2.4 collective-permute-done.1
  136.9 6.6 %collective-permute-start.2 = (bf16[16,2048]{1,0:T(8,128)(2,1)S(1)}, bf16[16,2048]{1,0:T(8,128)(2,1)S(1)}, u32[]{:S(2)}, u32[]{:S(2)}) collective-permute-start(bf16[16,2048]{1,0:T(8,128)(2,1)S(1)} %maximum_select_fusion.2), channel_id=1, source_target_pairs={{0,4},{1,5},{2,6},{3,7},{4,0},{5,1},{6,2},{7,3},{8,12},{9,13},{10,... | collective-permute-start | bytes 196616 | tf_op jit(solution)/shard_map/ppermute | solution.py:18
  143.5 50.7 %all-gather.7.cloned.1.call-done = bf16[4096,512]{1,0:T(8,128)(2,1)} async-done(((bf16[128,512]{1,0:T(8,128)(2,1)}), bf16[4096,512]{1,0:T(8,128)(2,1)}) %all-gather.7.cloned.1.call-update) | async-done | bytes 4194320 | tf_op jit(solution)/shard_map/all_gather | solution.py:136
  194.3 2.8 fusion.16
  197.8 7.0 %all-to-all-start = ((bf16[8,16,512]{2,1,0:T(8,128)(2,1)}), bf16[8,16,512]{2,1,0:T(8,128)(2,1)S(1)}, u32[]{:S(2)}, u32[]{:S(2)}) async-start(bf16[8,16,512]{2,1,0:T(8,128)(2,1)} %broadcast_in_dim.33), calls=%async_computation | async-start | bytes 262144 | tf_op jit(solution)/shard_map/all_to_all | solution.py:37
  204.8 8.0 %all-to-all-done = bf16[8,16,512]{2,1,0:T(8,128)(2,1)S(1)} async-done(((bf16[8,16,512]{2,1,0:T(8,128)(2,1)}), bf16[8,16,512]{2,1,0:T(8,128)(2,1)S(1)}, u32[]{:S(2)}, u32[]{:S(2)}) %all-to-all-start) | async-done | bytes 131104 | tf_op jit(solution)/shard_map/all_to_all | solution.py:37
  214.8 68.3 %all-gather.9.cloned.1.call-done = bf16[32,12,4096]{2,1,0:T(8,128)(2,1)} async-done(((bf16[1,12,4096]{2,1,0:T(8,128)(2,1)}), bf16[32,12,4096]{2,1,0:T(8,128)(2,1)}) %all-gather.9.cloned.1.call-update) | async-done | bytes 3145744 | tf_op jit(solution)/shard_map/all_gather | solution.py:166
  283.0 5.6 %reshape.160 = bf16[384,4096]{1,0:T(8,128)(2,1)} reshape(bf16[32,12,4096]{2,1,0:T(8,128)(2,1)} %all-gather.9.cloned.1.call-done) | data formatting | bytes 6291456
  288.6 2.9 fusion.30
  291.6 7.0 %convolution_convert_fusion = bf16[384,4096]{1,0:T(8,128)(2,1)} fusion(bf16[384,4096]{1,0:T(8,128)(2,1)} %reshape.160, bf16[1,128,4096]{2,1,0:T(8,128)(2,1)S(1)} %copy-done, bf16[1,4096,128]{2,1,0:T(8,128)(2,1)S(1)} %copy-done.2, f32[384,128]{1,0:T(8,128)S(1)} %fusion.30), kind=kOutput, calls=%fused_computation.2 | convolution fusion | flops 807174144 | bytes 8585216 | tf_op jit(solution)/shard_map/dot_general | solution.py:171
  298.6 5.5 %reshape_reshape.3 = bf16[16,2,12,4096]{3,2,1,0:T(8,128)(2,1)} reshape(bf16[384,4096]{1,0:T(8,128)(2,1)} %convolution_convert_fusion) | data formatting | bytes 6291456 | tf_op jit(solution)/shard_map/reshape;reshape | solution.py:55
  304.1 5.6 %copy.51 = bf16[2,16,12,4096]{3,1,0,2:T(8,128)(2,1)} copy(bf16[2,16,12,4096]{3,2,0,1:T(8,128)(2,1)} %bitcast.61) | data formatting | bytes 6291456 | tf_op jit(solution)/shard_map/transpose | solution.py:56
  309.8 19.6 %reduce-scatter.3.cloned.1.call-done = bf16[16,12,4096]{2,0,1:T(8,128)(2,1)} async-done(((bf16[32,12,4096]{2,0,1:T(8,128)(2,1)}), bf16[16,12,4096]{2,0,1:T(8,128)(2,1)}) %reduce-scatter.3.cloned.1.call-update) | async-done | bytes 1572880 | tf_op jit(solution)/shard_map/reduce_scatter | solution.py:59
  329.4 3.6 copy.52
  333.2 22.4 %all_gather.15 = bf16[32,1024]{1,0:T(8,128)(2,1)S(1)} all-gather(bf16[32,128]{1,0:T(8,128)(2,1)S(1)} %pad_maximum_fusion), channel_id=1, replica_groups=mesh['groups'=2,'seq_0'=16,'seq_1'=2,'rep'=8] {'rep'}, dimensions={1}, use_global_device_ids=true | all-gather | bytes 73728 | tf_op jit(solution)/shard_map/all_gather | solution.py:28
  356.2 54.9 %reduce-scatter.5.cloned.1.call-done = bf16[1,12,4096]{2,1,0:T(8,128)(2,1)} async-done(((bf16[16,12,4096]{2,1,0:T(8,128)(2,1)}), bf16[1,12,4096]{2,1,0:T(8,128)(2,1)}) %reduce-scatter.5.cloned.1.call-update) | async-done | bytes 98320 | tf_op jit(solution)/shard_map/reduce_scatter | solution.py:59
  412.7 7.4 %all-to-all-start.1 = ((bf16[12,8,512]{2,0,1:T(8,128)(2,1)}), bf16[12,8,512]{2,0,1:T(8,128)(2,1)S(1)}, u32[]{:S(2)}, u32[]{:S(2)}) async-start(bf16[12,8,512]{2,0,1:T(8,128)(2,1)} %copy.53), calls=%async_computation.3 | async-start | bytes 262144 | tf_op jit(solution)/shard_map/all_to_all | solution.py:176
  420.3 7.4 %all-to-all-done.1 = bf16[12,8,512]{2,0,1:T(8,128)(2,1)S(1)} async-done(((bf16[12,8,512]{2,0,1:T(8,128)(2,1)}), bf16[12,8,512]{2,0,1:T(8,128)(2,1)S(1)}, u32[]{:S(2)}, u32[]{:S(2)}) %all-to-all-start.1) | async-done | bytes 98336 | tf_op jit(solution)/shard_map/all_to_all | solution.py:176
  (69 shorter events, 11.8 us)
Async XLA Ops:
  7.2 284.4 %copy-start = (bf16[1,128,4096]{2,1,0:T(8,128)(2,1)S(1)}, bf16[1,128,4096]{2,1,0:T(8,128)(2,1)}, u32[]{:S(2)}) copy-start(bf16[1,128,4096]{2,1,0:T(8,128)(2,1)} %param.26) | copy-start | bytes 3145732
  7.2 112.7 %all-gather.5.cloned.1.call-start = ((), (), s32[]{:S(2)}) async-start(), calls=%async_computation.4 | async-start | bytes 4595712 | tf_op jit(solution)/shard_map/all_gather | solution.py:28
  9.0 185.3 %all-gather.7.cloned.1.call-start = ((), (), s32[]{:S(2)}) async-start(), calls=%async_computation.5 | async-start | bytes 4325376 | tf_op jit(solution)/shard_map/all_gather | solution.py:136
  119.9 3.7 copy-start.10
  123.6 70.7 %copy-start.6 = (bf16[16,512]{1,0:T(8,128)(2,1)S(1)}, bf16[16,512]{1,0:T(8,128)(2,1)}, u32[]{:S(2)}) copy-start(bf16[16,512]{1,0:T(8,128)(2,1)} %param.20) | copy-start | bytes 49156
  124.5 5.7 %collective-permute-start = (bf16[16,512]{1,0:T(8,128)(2,1)S(1)}, bf16[16,512]{1,0:T(8,128)(2,1)S(1)}, u32[]{:S(2)}, u32[]{:S(2)}) collective-permute-start(bf16[16,512]{1,0:T(8,128)(2,1)S(1)} %convert_element_type.81), channel_id=1, source_target_pairs={{0,1},{1,0},{2,3},{3,2},{4,5},{5,4},{6,7},{7,6},{8,9},{9,8},{10,11... | collective-permute-start | bytes 49160 | tf_op jit(solution)/shard_map/ppermute | solution.py:18
  130.2 6.7 %collective-permute-start.1 = (bf16[16,1024]{1,0:T(8,128)(2,1)S(1)}, bf16[16,1024]{1,0:T(8,128)(2,1)S(1)}, u32[]{:S(2)}, u32[]{:S(2)}) collective-permute-start(bf16[16,1024]{1,0:T(8,128)(2,1)S(1)} %maximum_select_fusion.3), channel_id=1, source_target_pairs={{0,2},{1,3},{2,0},{3,1},{4,6},{5,7},{6,4},{7,5},{8,10},{9,11},{10,... | collective-permute-start | bytes 98312 | tf_op jit(solution)/shard_map/ppermute | solution.py:18
  136.9 57.3 %collective-permute-start.2 = (bf16[16,2048]{1,0:T(8,128)(2,1)S(1)}, bf16[16,2048]{1,0:T(8,128)(2,1)S(1)}, u32[]{:S(2)}, u32[]{:S(2)}) collective-permute-start(bf16[16,2048]{1,0:T(8,128)(2,1)S(1)} %maximum_select_fusion.2), channel_id=1, source_target_pairs={{0,4},{1,5},{2,6},{3,7},{4,0},{5,1},{6,2},{7,3},{8,12},{9,13},{10,... | collective-permute-start | bytes 196616 | tf_op jit(solution)/shard_map/ppermute | solution.py:18
  143.5 61.3 %copy-start.9 = (s32[16,2]{0,1:T(2,128)S(1)}, s32[16,2]{0,1:T(2,128)}, u32[]{:S(2)}) copy-start(s32[16,2]{0,1:T(2,128)} %param.27) | copy-start | bytes 388
  143.5 69.5 %copy-start.4 = (f32[4096,4]{0,1:T(4,128)S(1)}, f32[4096,4]{0,1:T(4,128)}, u32[]{:S(2)}) copy-start(f32[4096,4]{0,1:T(4,128)} %param.23) | copy-start | bytes 196612
  143.5 69.5 %copy-start.5 = (f32[4096]{0:T(1024)S(1)}, f32[4096]{0:T(1024)}, u32[]{:S(2)}) copy-start(f32[4096]{0:T(1024)} %param.22) | copy-start | bytes 49156
  197.1 230.6 %copy-start.3 = (bf16[16,512]{1,0:T(8,128)(2,1)}, bf16[16,512]{1,0:T(8,128)(2,1)S(1)}, u32[]{:S(2)}) copy-start(bf16[16,512]{1,0:T(8,128)(2,1)S(1)} %fusion.16) | copy-start | bytes 49156
  197.8 15.0 %all-to-all-start = ((bf16[8,16,512]{2,1,0:T(8,128)(2,1)}), bf16[8,16,512]{2,1,0:T(8,128)(2,1)S(1)}, u32[]{:S(2)}, u32[]{:S(2)}) async-start(bf16[8,16,512]{2,1,0:T(8,128)(2,1)} %broadcast_in_dim.33), calls=%async_computation | async-start | bytes 262144 | tf_op jit(solution)/shard_map/all_to_all | solution.py:37
  204.8 78.2 %all-gather.9.cloned.1.call-start = ((), (), s32[]{:S(2)}) async-start(), calls=%async_computation.8 | async-start | bytes 4325376 | tf_op jit(solution)/shard_map/all_gather | solution.py:166
  214.7 74.0 %copy-start.1 = (bf16[1,4096,128]{2,1,0:T(8,128)(2,1)S(1)}, bf16[1,4096,128]{2,1,0:T(8,128)(2,1)}, u32[]{:S(2)}) copy-start(bf16[1,4096,128]{2,1,0:T(8,128)(2,1)} %param.24) | copy-start | bytes 3145732
  214.7 114.7 %reduce-scatter.3.cloned.1.call-start = ((), (), s32[]{:S(2)}) async-start(), calls=%async_computation.6 | async-start | bytes 4718592 | tf_op jit(solution)/shard_map/reduce_scatter | solution.py:59
  288.6 3.0 copy-start.2
  309.7 23.4 %copy-start.7 = (bf16[16,128]{1,0:T(8,128)(2,1)S(1)}, bf16[16,128]{1,0:T(8,128)(2,1)}, u32[]{:S(2)}) copy-start(bf16[16,128]{1,0:T(8,128)(2,1)} %param.16) | copy-start | bytes 12292
  309.7 23.4 %copy-start.8 = (bf16[16,128]{1,0:T(8,128)(2,1)S(1)}, bf16[16,128]{1,0:T(8,128)(2,1)}, u32[]{:S(2)}) copy-start(bf16[16,128]{1,0:T(8,128)(2,1)} %param.15) | copy-start | bytes 12292
  309.7 101.3 %reduce-scatter.5.cloned.1.call-start = ((), (), s32[]{:S(2)}) async-start(), calls=%async_computation.7 | async-start | bytes 2228224 | tf_op jit(solution)/shard_map/reduce_scatter | solution.py:59
  412.7 15.0 %all-to-all-start.1 = ((bf16[12,8,512]{2,0,1:T(8,128)(2,1)}), bf16[12,8,512]{2,0,1:T(8,128)(2,1)S(1)}, u32[]{:S(2)}, u32[]{:S(2)}) async-start(bf16[12,8,512]{2,0,1:T(8,128)(2,1)} %copy.53), calls=%async_computation.3 | async-start | bytes 262144 | tf_op jit(solution)/shard_map/all_to_all | solution.py:176
Sparse Core Ops, SparseCore 0:
  10.2 109.7 all-gather.4
  122.1 72.1 all-gather.6
  214.8 68.1 all-gather.8
  309.8 19.5 reduce-scatter.2
  333.3 77.7 reduce-scatter.4
